TPU v7x, 32 devices: a whole 2x2x4 slice. The times are simulated.
32 devices in a mesh: sample: 4 (over y, x), gz: 8 (over z, core).
Axes of the slice: x: 2, y: 2, z: 4, core: 2. Of those that a mesh axis runs over, the one named last changes fastest.
Arguments:
- field_now: float32 [12, 16, 160, 256], P('sample', 'gz'), parts along dimension 0, may hold values from -6 to 6
- field_before: float32 [12, 16, 160, 256], P('sample', 'gz'), parts along dimension 0, may hold values from -6 to 6
- lame_lambda: float32 [16, 640, 256], P('gz', 'sample'), parts along dimension 1, may hold values from 0.5 to 1.5
- shear_modulus: float32 [16, 640, 256], P('gz', 'sample'), parts along dimension 1, may hold values from 0.5 to 1.5
- density: float32 [16, 640, 256], P('gz', 'sample'), parts along dimension 1, may hold values from 1 to 2
- source_field: float32 [12, 16, 160, 256], P('sample', 'gz'), parts along dimension 0, may hold values from -6 to 6
- wavelet: float32 [32], P('sample'), parts along dimension 0, may hold values from -4 to 4
- prior_mean: float32 [16, 640, 256], P('gz', 'sample'), parts along dimension 1, may hold values from 0.5 to 1.5
- steps_taken: float32 [16, 16, 160, 256], P('sample', 'gz'), parts along dimension 0
- grad_change: float32 [16, 16, 160, 256], P('sample', 'gz'), parts along dimension 0, as said below
Outputs:
- field_final: float32 [12, 16, 160, 256], P('sample', 'gz'), parts along dimension 0
- gradient: float32 [16, 640, 256], P('gz', 'sample'), parts along dimension 1
- direction: float32 [16, 640, 256], P('gz', 'sample'), parts along dimension 1
There are 4 independent parts, one for each index of `sample`. A program takes and returns all parts, laid end to end along the dimension named above; each array names one. Nothing has to cross between parts.
Inputs may be any that keep to these rules, and one draw needn't show every extreme that they name: Each entry of grad_change is 0.5 to 2 times the matching entry of steps_taken.
All inputs are finite; a program needn't handle non-finite values.
Results may differ from a plain program's by a relative error of at most 0.0003.
Values sent between devices are 32-bit elements; how exact they have to be, the bound alone decides.
A program may use at most 64 MiB of HBM per device.

v0:
```python
import functools

import jax
import jax.numpy as jnp
from jax import lax
from jax.experimental import pallas as pl
from jax.experimental.pallas import tpu as pltpu
from jax.sharding import PartitionSpec as P

PAD = 8
CHUNK_ROWS = 16


def chunk_rows(rows):
    size = CHUNK_ROWS
    while rows % size:
        size //= 2
    return size


def tile(start):
    return pl.ds(pl.multiple_of(start, 8), 8)


def kernel(
    n,
    steps,
    pairs,
    size,
    now_hbm,
    before_hbm,
    lame_hbm,
    shear_hbm,
    density_hbm,
    source_hbm,
    wavelet,
    prior_hbm,
    taken_hbm,
    change_hbm,
    final_hbm,
    gradient_hbm,
    direction_hbm,
    even,
    odd,
    lame,
    shear,
    coeff,
    source,
    prior,
    taken,
    change,
    grad,
    direction,
    sums,
    part,
    gathered,
    load_sem,
    store_sem,
    send_sem,
    recv_sem,
    part_send,
    part_recv,
):
    me = lax.axis_index("gz")
    rows, cols = lame.shape[1], lame.shape[2]
    chunks = rows // size
    tiles = size // 8
    has_low = me > 0
    has_high = me < n - 1
    inside = pl.ds(PAD, rows)

    loads = [
        pltpu.make_async_copy(src, dst, load_sem.at[i])
        for i, (src, dst) in enumerate(
            (
                (now_hbm, even.at[:, pl.ds(1, 2), inside]),
                (lame_hbm, lame),
                (shear_hbm, shear),
                (density_hbm, coeff),
                (before_hbm, odd.at[:, pl.ds(1, 2), inside]),
                (source_hbm, source),
                (taken_hbm, taken),
                (change_hbm, change),
                (prior_hbm, prior),
            )
        )
    ]
    for load in loads:
        load.start()

    barrier = pltpu.get_barrier_semaphore()
    for k in range(1, n):
        pl.semaphore_signal(
            barrier,
            inc=1,
            device_id={"gz": lax.rem(me + k, n)},
            device_id_type=pl.DeviceIdType.MESH,
        )

    edge = jnp.zeros((even.shape[0], 4, PAD, cols), jnp.float32)
    for ref in (even, odd):
        ref[:, :, pl.ds(0, PAD)] = edge
        ref[:, :, pl.ds(PAD + rows, PAD)] = edge

    def clear(plane):
        def body(t, carry):
            for ref in (even, odd):
                for comp in range(3):
                    ref[comp, plane, tile(PAD + 8 * t)] = jnp.zeros((8, cols), jnp.float32)
            return carry

        lax.fori_loop(0, rows // 8, body, 0)

    @pl.when(me == 0)
    def _():
        clear(0)

    @pl.when(me == n - 1)
    def _():
        clear(3)

    def rdma(ref, parity, up, chunk):
        where = pl.ds(pl.multiple_of(PAD + chunk * size, 8), size)
        side = 0 if up else 1
        target = lax.rem(me + (1 if up else n - 1), n)
        return pltpu.make_async_remote_copy(
            src_ref=ref.at[:, 2 if up else 1, where],
            dst_ref=ref.at[:, 0 if up else 3, where],
            send_sem=send_sem.at[parity, side, chunk],
            recv_sem=recv_sem.at[parity, side, chunk],
            device_id={"gz": target},
            device_id_type=pl.DeviceIdType.MESH,
        )

    def send(ref, parity, chunk):
        @pl.when(has_high)
        def _():
            rdma(ref, parity, True, chunk).start()

        @pl.when(has_low)
        def _():
            rdma(ref, parity, False, chunk).start()

    def sent(ref, parity, chunk):
        @pl.when(has_high)
        def _():
            rdma(ref, parity, True, chunk).wait_send()

        @pl.when(has_low)
        def _():
            rdma(ref, parity, False, chunk).wait_send()

    def received(ref, parity, chunk):
        @pl.when(has_low)
        def _():
            rdma(ref, parity, True, chunk).wait_recv()

        @pl.when(has_high)
        def _():
            rdma(ref, parity, False, chunk).wait_recv()

    loads[0].wait()
    pl.semaphore_wait(barrier, n - 1)

    def first(chunk, carry):
        send(even, 0, chunk)
        return carry

    lax.fori_loop(0, chunks, first, 0)

    for load in loads[1:4]:
        load.wait()

    def prepare(t, carry):
        for plane in range(2):
            at = (plane, tile(8 * t))
            lame[at] = lame[at] + shear[at]
            coeff[at] = 0.04 / coeff[at]
            grad[at] = jnp.zeros((8, cols), jnp.float32)
        return carry

    lax.fori_loop(0, rows // 8, prepare, 0)
    for load in loads[4:]:
        load.wait()

    half = cols // 2
    products = [(i, pairs + j) for i in range(pairs) for j in range(pairs)]
    products += [(pairs + i, pairs + j) for i in range(pairs) for j in range(i, pairs)]
    count = len(products)
    where_of = {pair: k for k, pair in enumerate(products)}
    for i in range(2 * pairs):
        where_of[(i, 2 * pairs)] = count + i

    def fold(value):
        out = value[:, 0:128]
        for k in range(1, cols // 128):
            out = out + value[:, 128 * k : 128 * (k + 1)]
        return out

    def stored(t, totals):
        totals = list(totals)
        for plane in range(2):
            vectors = [taken[i, plane, tile(8 * t)] for i in range(pairs)]
            vectors += [change[i, plane, tile(8 * t)] for i in range(pairs)]
            for k, (a, b) in enumerate(products):
                totals[k] = totals[k] + fold(vectors[a] * vectors[b])
        return tuple(totals)

    totals = lax.fori_loop(
        0, rows // 8, stored, tuple(jnp.zeros((8, 128), jnp.float32) for _ in products)
    )
    place = lax.broadcasted_iota(jnp.int32, (1, 128), 1)

    def whole(value):
        return jnp.sum(jnp.sum(value, axis=0, keepdims=True), axis=1, keepdims=True)

    line = jnp.zeros((1, 128), jnp.float32)
    for k in range(count):
        line = jnp.where(place == k, whole(totals[k]), line)
    part[...] = line
    for i in range(2 * pairs):
        sums[i] = jnp.zeros((8, 128), jnp.float32)

    row_at = lax.broadcasted_iota(jnp.int32, (8, cols), 0)
    col_at = lax.broadcasted_iota(jnp.int32, (8, cols), 1)
    is_top, is_bottom = row_at == 0, row_at == 7
    is_left, is_right = col_at == 0, col_at == cols - 1

    def along_x(previous, value, following):
        minus = pltpu.roll(jnp.where(is_bottom, previous, value), 1, 0)
        plus = pltpu.roll(jnp.where(is_top, following, value), 7, 0)
        return minus, plus

    def along_y(value):
        minus = jnp.where(is_left, 0.0, pltpu.roll(value, 1, 1))
        plus = jnp.where(is_right, 0.0, pltpu.roll(value, cols - 1, 1))
        return minus, plus

    def delta_y(value):
        minus, plus = along_y(value)
        return plus - minus

    def update(step, current, other, t):
        amplitude = wavelet[step]

        def load(comp, plane, shift=0):
            return current[comp, plane, tile(PAD + 8 * (t + shift))]

        for plane in range(2):
            low, mid, high = plane, plane + 1, plane + 2
            at = tile(8 * t)
            here = tile(PAD + 8 * t)

            def delta_z(comp, shift=0):
                return load(comp, high, shift) - load(comp, low, shift)

            def delta_xz(comp, centre):
                minus, plus = along_x(delta_z(comp, -1), centre, delta_z(comp, 1))
                return plus - minus

            centre = [load(comp, mid) for comp in range(3)]
            diff = [delta_z(comp) for comp in range(3)]
            total = [load(comp, high) + load(comp, low) for comp in range(3)]
            xs = [along_x(load(comp, mid, -1), centre[comp], load(comp, mid, 1)) for comp in range(3)]
            ys = [along_y(centre[comp]) for comp in range(3)]
            sum_x = [minus + plus for minus, plus in xs]
            sum_y = [minus + plus for minus, plus in ys]
            dx = [plus - minus for minus, plus in xs]
            lap = [
                (total[comp] + sum_x[comp]) + (sum_y[comp] - 6.0 * centre[comp])
                for comp in range(3)
            ]
            mixed = [
                delta_xz(1, diff[1]) + delta_y(diff[2]),
                delta_xz(0, diff[0]) + delta_y(dx[2]),
                delta_y(diff[0] + dx[1]),
            ]
            own = [total[0], sum_x[1], sum_y[2]]
            both = lame[plane, at]
            mu = shear[plane, at]
            rate = coeff[plane, at]
            grad[plane, at] = grad[plane, at] + (
                centre[0] * lap[0] + centre[1] * lap[1] + centre[2] * lap[2]
            )
            for comp in range(3):
                doubled = 2.0 * centre[comp]
                elastic = both * ((own[comp] - doubled) + 0.25 * mixed[comp]) + mu * lap[comp]
                other[comp, mid, here] = (
                    doubled
                    - other[comp, mid, here]
                    + rate * (elastic + amplitude * source[comp, plane, at])
                )

    def finish(t, totals):
        totals = list(totals)
        for plane in range(2):
            at = (plane, tile(8 * t))
            value = (shear[at] - prior[at]) + 0.02 * grad[at]
            grad[at] = value
            for i in range(pairs):
                totals[i] = totals[i] + fold(taken[(i,) + at] * value)
                totals[pairs + i] = totals[pairs + i] + fold(change[(i,) + at] * value)
        return tuple(totals)

    def advance(step, current, other, parity):
        received(current, parity, 0)

        def chunk_body(chunk, carry):
            @pl.when(chunk + 1 < chunks)
            def _():
                received(current, parity, chunk + 1)

            @pl.when(step > 0)
            def _():
                sent(other, 1 - parity, chunk)

            def tile_body(t, inner):
                update(step, current, other, chunk * tiles + t)
                return inner

            lax.fori_loop(0, tiles, tile_body, 0)

            @pl.when(step < steps - 1)
            def _():
                send(other, 1 - parity, chunk)

            if parity == 1:

                @pl.when(step == steps - 1)
                def _():
                    totals = lax.fori_loop(
                        chunk * tiles,
                        chunk * tiles + tiles,
                        finish,
                        tuple(sums[i] for i in range(2 * pairs)),
                    )
                    for i in range(2 * pairs):
                        sums[i] = totals[i]

            return carry

        lax.fori_loop(0, chunks, chunk_body, 0)

    def two_steps(k, carry):
        advance(2 * k, even, odd, 0)
        advance(2 * k + 1, odd, even, 1)
        return carry

    lax.fori_loop(0, steps // 2, two_steps, 0)

    line = part[...]
    for i in range(2 * pairs):
        line = jnp.where(place == count + i, whole(sums[i]), line)
    part[...] = line

    outs = [
        pltpu.make_async_copy(grad, gradient_hbm, store_sem.at[0]),
        pltpu.make_async_copy(even.at[:, pl.ds(1, 2), inside], final_hbm, store_sem.at[1]),
        pltpu.make_async_copy(direction, direction_hbm, store_sem.at[2]),
    ]
    exchange = [
        pltpu.make_async_remote_copy(
            src_ref=part,
            dst_ref=gathered.at[k - 1],
            send_sem=part_send.at[k - 1],
            recv_sem=part_recv.at[k - 1],
            device_id={"gz": lax.rem(me + k, n)},
            device_id_type=pl.DeviceIdType.MESH,
        )
        for k in range(1, n)
    ]
    for copy in exchange:
        copy.start()
    outs[0].start()
    outs[1].start()

    def last_sent(chunk, carry):
        sent(odd, 1, chunk)
        return carry

    lax.fori_loop(0, chunks, last_sent, 0)
    for copy in exchange:
        copy.wait_recv()
    line = part[...]
    for k in range(n - 1):
        line = line + gathered[k]

    def product(a, b):
        k = where_of[(min(a, b), max(a, b))]
        return jnp.sum(jnp.where(place == k, line, 0.0), axis=1, keepdims=True)

    cache = {}

    def inner(a, b):
        key = (min(a, b), max(a, b))
        if key not in cache:
            cache[key] = product(*key)
        return cache[key]

    gradient_at = 2 * pairs
    curvature = [inner(i, pairs + i) for i in range(pairs)]
    alphas = [None] * pairs
    for i in reversed(range(pairs)):
        value = inner(i, gradient_at)
        for j in range(i + 1, pairs):
            value = value - alphas[j] * inner(i, pairs + j)
        alphas[i] = value / curvature[i]
    newest = 2 * pairs - 1
    gamma = curvature[pairs - 1] / inner(newest, newest)
    changes = [-gamma * alphas[i] for i in range(pairs)]
    steps_coef = [None] * pairs
    for i in range(pairs):
        value = gamma * inner(pairs + i, gradient_at)
        for j in range(pairs):
            value = value + changes[j] * inner(pairs + i, pairs + j)
        for j in range(i):
            value = value + steps_coef[j] * inner(j, pairs + i)
        steps_coef[i] = alphas[i] - value / curvature[i]

    def spread(value):
        return -jnp.broadcast_to(value, (8, cols))

    by_grad = spread(gamma)
    by_taken = [spread(value) for value in steps_coef]
    by_change = [spread(value) for value in changes]

    def combine(t, carry):
        for plane in range(2):
            at = (plane, tile(8 * t))
            value = by_grad * grad[at]
            for i in range(pairs):
                value = value + by_taken[i] * taken[(i,) + at]
                value = value + by_change[i] * change[(i,) + at]
            direction[at] = value
        return carry

    lax.fori_loop(0, rows // 8, combine, 0)
    outs[2].start()
    for copy in exchange:
        copy.wait_send()
    for out in outs:
        out.wait()


def on_device(
    n,
    field_now,
    field_before,
    lame_lambda,
    shear_modulus,
    density,
    source_field,
    wavelet,
    prior_mean,
    steps_taken,
    grad_change,
):
    comps, depth, rows, cols = field_now.shape
    pairs = steps_taken.shape[0]
    steps = wavelet.shape[0]
    size = chunk_rows(rows)
    chunks = rows // size
    f32 = jnp.float32
    state = pltpu.VMEM((comps, depth + 2, rows + 2 * PAD, cols), f32)
    model = pltpu.VMEM((depth, rows, cols), f32)
    stored = pltpu.VMEM((pairs, depth, rows, cols), f32)
    dma = pltpu.SemaphoreType.DMA
    anywhere = pl.BlockSpec(memory_space=pl.ANY)
    return pl.pallas_call(
        functools.partial(kernel, n, steps, pairs, size),
        out_shape=(
            jax.ShapeDtypeStruct(field_now.shape, f32),
            jax.ShapeDtypeStruct(lame_lambda.shape, f32),
            jax.ShapeDtypeStruct(lame_lambda.shape, f32),
        ),
        in_specs=[anywhere] * 6
        + [pl.BlockSpec(memory_space=pltpu.SMEM)]
        + [anywhere] * 3,
        out_specs=(anywhere, anywhere, anywhere),
        scratch_shapes=[
            state,
            state,
            model,
            model,
            model,
            pltpu.VMEM((comps, depth, rows, cols), f32),
            model,
            stored,
            stored,
            model,
            model,
            pltpu.VMEM((2 * pairs, 8, 128), f32),
            pltpu.VMEM((1, 128), f32),
            pltpu.VMEM((n - 1, 1, 128), f32),
            dma((9,)),
            dma((3,)),
            dma((2, 2, chunks)),
            dma((2, 2, chunks)),
            dma((n - 1,)),
            dma((n - 1,)),
        ],
        compiler_params=pltpu.CompilerParams(
            collective_id=0, has_side_effects=True, vmem_limit_bytes=48 * 1024 * 1024
        ),
    )(
        field_now,
        field_before,
        lame_lambda,
        shear_modulus,
        density,
        source_field,
        wavelet,
        prior_mean,
        steps_taken,
        grad_change,
    )


def solution(mesh):
    n = mesh.shape["gz"]
    fields = P("sample", "gz", None, None)
    models = P("gz", "sample", None)
    placed = (
        fields,
        fields,
        models,
        models,
        models,
        fields,
        P("sample"),
        models,
        fields,
        fields,
    )
    return jax.shard_map(
        functools.partial(on_device, n),
        mesh=mesh,
        in_specs=placed,
        out_specs=(fields, models, models),
        check_vma=False,
    )
```

profile of v0, /device:TPU:0, one launch (start us, length us, event | category | flops | bytes accessed | tf_op | source)
XLA Modules:
  0.0 66.7 jit_solution(14509130188422830940)
XLA Ops:
  0.6 0.0 copy-start
  0.6 1.2 %copy-done = f32[3,2,160,256]{3,2,1,0:T(8,128)S(1)} copy-done((f32[3,2,160,256]{3,2,1,0:T(8,128)S(1)}, f32[3,2,160,256]{3,2,1,0:T(8,128)}, u32[]{:S(2)}) %copy-start) | copy-done | bytes 983064
  1.8 0.0 copy-start.1
  1.8 1.2 %copy-done.1 = f32[3,2,160,256]{3,2,1,0:T(8,128)S(1)} copy-done((f32[3,2,160,256]{3,2,1,0:T(8,128)S(1)}, f32[3,2,160,256]{3,2,1,0:T(8,128)}, u32[]{:S(2)}) %copy-start.1) | copy-done | bytes 983064
  3.0 0.0 copy-start.2
  3.0 1.2 %copy-done.2 = f32[3,2,160,256]{3,2,1,0:T(8,128)S(1)} copy-done((f32[3,2,160,256]{3,2,1,0:T(8,128)S(1)}, f32[3,2,160,256]{3,2,1,0:T(8,128)}, u32[]{:S(2)}) %copy-start.2) | copy-done | bytes 983064
  4.2 0.0 copy-start.3
  4.2 1.0 %copy-done.3 = f32[2,160,256]{2,1,0:T(8,128)S(1)} copy-done((f32[2,160,256]{2,1,0:T(8,128)S(1)}, f32[2,160,256]{2,1,0:T(8,128)}, u32[]{:S(2)}) %copy-start.3) | copy-done | bytes 327704
  5.2 0.0 copy-start.4
  5.2 1.0 %copy-done.4 = f32[2,160,256]{2,1,0:T(8,128)S(1)} copy-done((f32[2,160,256]{2,1,0:T(8,128)S(1)}, f32[2,160,256]{2,1,0:T(8,128)}, u32[]{:S(2)}) %copy-start.4) | copy-done | bytes 327704
  6.2 0.0 copy-start.5
  6.2 1.0 %copy-done.5 = f32[2,160,256]{2,1,0:T(8,128)S(1)} copy-done((f32[2,160,256]{2,1,0:T(8,128)S(1)}, f32[2,160,256]{2,1,0:T(8,128)}, u32[]{:S(2)}) %copy-start.5) | copy-done | bytes 327704
  7.2 0.0 copy-start.6
  7.2 1.0 %copy-done.6 = f32[2,160,256]{2,1,0:T(8,128)S(1)} copy-done((f32[2,160,256]{2,1,0:T(8,128)S(1)}, f32[2,160,256]{2,1,0:T(8,128)}, u32[]{:S(2)}) %copy-start.6) | copy-done | bytes 327704
  8.1 0.0 copy-start.7
  8.1 0.7 copy-done.7
  8.8 55.5 %shard_map.121 = (f32[3,2,160,256]{3,2,1,0:T(8,128)S(1)}, f32[2,160,256]{2,1,0:T(8,128)S(1)}, f32[2,160,256]{2,1,0:T(8,128)S(1)}) custom-call(f32[3,2,160,256]{3,2,1,0:T(8,128)S(1)} %copy-done, f32[3,2,160,256]{3,2,1,0:T(8,128)S(1)} %copy-done.1, f32[2,160,256]{2,1,0:T(8,128)S(1)} %copy-done.3, f32[2,160,256]{2,1,0:T(8,128)S(1)} %copy-done.4, ...), custom_call_target="tpu_custom_call" | custom-call | tf_op jit(solution)/shard_map/pallas_call | solution.py:469
  64.3 0.9 %copy.16 = f32[3,2,160,256]{3,2,1,0:T(8,128)} copy(f32[3,2,160,256]{3,2,1,0:T(8,128)S(1)} %get-tuple-element.6) | data formatting | bytes 1966080
  65.2 0.7 %copy.17 = f32[2,160,256]{2,1,0:T(8,128)} copy(f32[2,160,256]{2,1,0:T(8,128)S(1)} %get-tuple-element.7) | data formatting | bytes 655360
  66.0 0.7 %copy.18 = f32[2,160,256]{2,1,0:T(8,128)} copy(f32[2,160,256]{2,1,0:T(8,128)S(1)} %get-tuple-element.8) | data formatting | bytes 655360
Async XLA Ops:
  0.6 1.2 %copy-start = (f32[3,2,160,256]{3,2,1,0:T(8,128)S(1)}, f32[3,2,160,256]{3,2,1,0:T(8,128)}, u32[]{:S(2)}) copy-start(f32[3,2,160,256]{3,2,1,0:T(8,128)} %now_hbm.1) | copy-start | bytes 2949124
  1.8 1.2 %copy-start.1 = (f32[3,2,160,256]{3,2,1,0:T(8,128)S(1)}, f32[3,2,160,256]{3,2,1,0:T(8,128)}, u32[]{:S(2)}) copy-start(f32[3,2,160,256]{3,2,1,0:T(8,128)} %before_hbm.1) | copy-start | bytes 2949124
  3.0 1.2 %copy-start.2 = (f32[3,2,160,256]{3,2,1,0:T(8,128)S(1)}, f32[3,2,160,256]{3,2,1,0:T(8,128)}, u32[]{:S(2)}) copy-start(f32[3,2,160,256]{3,2,1,0:T(8,128)} %source_hbm.1) | copy-start | bytes 2949124
  4.2 1.0 %copy-start.3 = (f32[2,160,256]{2,1,0:T(8,128)S(1)}, f32[2,160,256]{2,1,0:T(8,128)}, u32[]{:S(2)}) copy-start(f32[2,160,256]{2,1,0:T(8,128)} %lame_hbm.1) | copy-start | bytes 983044
  5.2 1.0 %copy-start.4 = (f32[2,160,256]{2,1,0:T(8,128)S(1)}, f32[2,160,256]{2,1,0:T(8,128)}, u32[]{:S(2)}) copy-start(f32[2,160,256]{2,1,0:T(8,128)} %shear_hbm.1) | copy-start | bytes 983044
  6.2 1.0 %copy-start.5 = (f32[2,160,256]{2,1,0:T(8,128)S(1)}, f32[2,160,256]{2,1,0:T(8,128)}, u32[]{:S(2)}) copy-start(f32[2,160,256]{2,1,0:T(8,128)} %density_hbm.1) | copy-start | bytes 983044
  7.2 1.0 %copy-start.6 = (f32[2,160,256]{2,1,0:T(8,128)S(1)}, f32[2,160,256]{2,1,0:T(8,128)}, u32[]{:S(2)}) copy-start(f32[2,160,256]{2,1,0:T(8,128)} %prior_hbm.1) | copy-start | bytes 983044
  8.1 0.7 copy-start.7
where the time goes:
time: 67.1 us; the launch traced here: 66.7 us
  Pallas kernels  55.5 us (83%)
  local copies, waits for them, and re-layouts  10.5 us (16%)
    pallas_call x1, Pallas kernels, on_device(): pl.pallas_call(functools.partial(kernel, n, steps, pairs, size), out_shap...  55.5 us
    unnamed x19, local copies, waits for them, and re-layouts  10.5 us

commit v1 on v0

--- a/solution.py
+++ b/solution.py
@@ -38,8 +38,8 @@
     taken_hbm,
     change_hbm,
     final_hbm,
-    gradient_hbm,
-    direction_hbm,
+    grad,
+    direction,
     even,
     odd,
     lame,
@@ -49,8 +49,6 @@
     prior,
     taken,
     change,
-    grad,
-    direction,
     sums,
     part,
     gathered,
@@ -353,11 +351,7 @@
         line = jnp.where(place == count + i, whole(sums[i]), line)
     part[...] = line
 
-    outs = [
-        pltpu.make_async_copy(grad, gradient_hbm, store_sem.at[0]),
-        pltpu.make_async_copy(even.at[:, pl.ds(1, 2), inside], final_hbm, store_sem.at[1]),
-        pltpu.make_async_copy(direction, direction_hbm, store_sem.at[2]),
-    ]
+    out = pltpu.make_async_copy(even.at[:, pl.ds(1, 2), inside], final_hbm, store_sem.at[0])
     exchange = [
         pltpu.make_async_remote_copy(
             src_ref=part,
@@ -371,8 +365,7 @@
     ]
     for copy in exchange:
         copy.start()
-    outs[0].start()
-    outs[1].start()
+    out.start()
 
     def last_sent(chunk, carry):
         sent(odd, 1, chunk)
@@ -435,11 +428,9 @@
         return carry
 
     lax.fori_loop(0, rows // 8, combine, 0)
-    outs[2].start()
     for copy in exchange:
         copy.wait_send()
-    for out in outs:
-        out.wait()
+    out.wait()
 
 
 def on_device(
@@ -465,18 +456,19 @@
     model = pltpu.VMEM((depth, rows, cols), f32)
     stored = pltpu.VMEM((pairs, depth, rows, cols), f32)
     dma = pltpu.SemaphoreType.DMA
-    anywhere = pl.BlockSpec(memory_space=pl.ANY)
-    return pl.pallas_call(
+    anywhere = pl.BlockSpec(memory_space=pltpu.HBM)
+    free = pl.BlockSpec(memory_space=pl.ANY)
+    results = pl.pallas_call(
         functools.partial(kernel, n, steps, pairs, size),
         out_shape=(
-            jax.ShapeDtypeStruct(field_now.shape, f32),
-            jax.ShapeDtypeStruct(lame_lambda.shape, f32),
-            jax.ShapeDtypeStruct(lame_lambda.shape, f32),
+            pltpu.VMEM(field_now.shape, f32),
+            pltpu.VMEM(lame_lambda.shape, f32),
+            pltpu.VMEM(lame_lambda.shape, f32),
         ),
         in_specs=[anywhere] * 6
         + [pl.BlockSpec(memory_space=pltpu.SMEM)]
         + [anywhere] * 3,
-        out_specs=(anywhere, anywhere, anywhere),
+        out_specs=(pl.BlockSpec(memory_space=pltpu.VMEM),) * 3,
         scratch_shapes=[
             state,
             state,
@@ -487,20 +479,18 @@
             model,
             stored,
             stored,
-            model,
-            model,
             pltpu.VMEM((2 * pairs, 8, 128), f32),
             pltpu.VMEM((1, 128), f32),
             pltpu.VMEM((n - 1, 1, 128), f32),
             dma((9,)),
-            dma((3,)),
+            dma((1,)),
             dma((2, 2, chunks)),
             dma((2, 2, chunks)),
             dma((n - 1,)),
             dma((n - 1,)),
         ],
         compiler_params=pltpu.CompilerParams(
-            collective_id=0, has_side_effects=True, vmem_limit_bytes=48 * 1024 * 1024
+            collective_id=0, has_side_effects=True, vmem_limit_bytes=65000000
         ),
     )(
         field_now,
@@ -514,6 +504,23 @@
         steps_taken,
         grad_change,
     )
+    return pl.pallas_call(
+        publish,
+        out_shape=tuple(jax.ShapeDtypeStruct(value.shape, f32) for value in results),
+        in_specs=[free] * 3,
+        out_specs=(free, free, free),
+        scratch_shapes=[dma((3,))],
+        compiler_params=pltpu.CompilerParams(vmem_limit_bytes=1024 * 1024),
+    )(*[pltpu.with_memory_space_constraint(value, pltpu.VMEM) for value in results])
+
+
+def publish(*refs):
+    sem = refs[-1]
+    copies = [pltpu.make_async_copy(refs[i], refs[3 + i], sem.at[i]) for i in range(3)]
+    for copy in copies:
+        copy.start()
+    for copy in copies:
+        copy.wait()
 
 
 def solution(mesh):

time: 67.1 us -> 56.6 us (0.84)
  local copies, waits for them, and re-layouts: 10.5 us -> 0 us
    unnamed x19 -> x0, local copies, waits for them, and re-layouts: 10.5 us -> none
    pallas_call x0 -> x1, Pallas kernels: none -> 1.18 us  [on_device(): pl.pallas_call(publish, out_shape=tuple((jax.ShapeDtypeStruct(value.shape...]
    pallas_call x1, Pallas kernels: 55.5 us -> 54.6 us  [on_device(): pl.pallas_call(functools.partial(kernel, n, steps, pairs, size), out_shap...]
where the time goes in v1:
time: 56.6 us; the launch traced here: 56.4 us
  Pallas kernels  55.8 us (99%)
  between operations  0.64 us (1%)
    pallas_call x1, Pallas kernels, on_device(): pl.pallas_call(functools.partial(kernel, n, steps, pairs, size), out_shap...  54.6 us
    pallas_call x1, Pallas kernels, on_device(): pl.pallas_call(publish, out_shape=tuple((jax.ShapeDtypeStruct(value.shape...  1.18 us

profile of v1, /device:TPU:0, one launch (start us, length us, event | category | flops | bytes accessed | tf_op | source)
XLA Modules:
  0.0 56.4 jit_solution(16692613304213532604)
XLA Ops:
  0.6 54.6 %shard_map.121 = (f32[3,2,160,256]{3,2,1,0:T(8,128)S(1)}, f32[2,160,256]{2,1,0:T(8,128)S(1)}, f32[2,160,256]{2,1,0:T(8,128)S(1)}) custom-call(f32[3,2,160,256]{3,2,1,0:T(8,128)} %now_hbm.1, f32[3,2,160,256]{3,2,1,0:T(8,128)} %before_hbm.1, f32[2,160,256]{2,1,0:T(8,128)} %lame_hbm.1, f32[2,160,256]{2,1,0:T(8,128)} %shear_hbm.1, f32[2,160,256]{2,1,0:T(8,128)} %density_hbm.1, ...), custom_call_target="tpu_custom_call" | custom-call | tf_op jit(solution)/shard_map/pallas_call | solution.py:461
  55.3 1.2 %shard_map.122 = (f32[3,2,160,256]{3,2,1,0:T(8,128)}, f32[2,160,256]{2,1,0:T(8,128)}, f32[2,160,256]{2,1,0:T(8,128)}) custom-call(f32[3,2,160,256]{3,2,1,0:T(8,128)S(1)} %get-tuple-element.6.refs_0_, f32[2,160,256]{2,1,0:T(8,128)S(1)} %get-tuple-element.7.refs_1_, f32[2,160,256]{2,1,0:T(8,128)S(1)} %get-tuple-element.8.refs_2_), custom_call_target="tpu_custom_call" | custom-call | tf_op jit(solution)/shard_map/pallas_call | solution.py:507
